TPU v7x, 32 devices: a whole 2x2x4 slice. The times are simulated.
32 devices in a mesh: freq: 8 (over z, y), cell: 4 (over x, core).
Axes of the slice: x: 2, y: 2, z: 4, core: 2. Of those that a mesh axis runs over, the one named last changes fastest.
Arguments:
- columns: float32 [2, 16, 64, 600], P(None, 'freq'), may hold values from -6 to 6
- freq_blocks: float32 [2, 16, 600, 1024], P(None, 'freq', None, 'cell'), may hold values from -0.1875 to 0.1875
- causal_cutoffs: int32 [64], replicated, may hold values from 3 to 15
- band_index: int32 [1024], P('cell'), may hold values from 0 to 7
- band_rates: float32 [8], replicated, may hold values from 0.05 to 0.45
Outputs:
- hessian_columns: float32 [2, 16, 64, 600], P(None, 'freq', 'cell')
All inputs are finite; a program needn't handle non-finite values.
Results may differ from a plain program's by a relative error of at most 0.00007.
Values sent between devices are 32-bit elements; how exact they have to be, the bound alone decides.
No kernel may reach another device: no remote copies, remote signals or barrier semaphores. Data moves between devices by JAX's collectives and lax.ppermute only.
A program may use at most 64 MiB of HBM per device.

v0:
```python
import math
import jax
import jax.numpy as jnp
from jax import lax
from jax.sharding import PartitionSpec as P

MODE_SHARE_WIDTH = 8
C_DEV = 256
SWEEPS = 4
BANDS = 8
precise = lax.Precision.HIGHEST


def extended(shard, sides, width):
    for axis, dim in sides:
        devices, length = (lax.axis_size(axis), shard.shape[dim])
        up = [(i, (i + 1) % devices) for i in range(devices - 1)]
        down = [(j, i) for i, j in up]
        last = lax.slice_in_dim(shard, length - width, length, axis=dim)
        leading = lax.slice_in_dim(shard, 0, width, axis=dim)
        before = lax.ppermute(last, axis, up)
        after = lax.ppermute(leading, axis, down)
        shard = jnp.concatenate([before, shard, after], axis=dim)
    return shard


def inverse_table(epoch_number, harmonic_number):
    cycle_length = 2 * epoch_number
    sample_moments = lax.broadcasted_iota(jnp.int32, (epoch_number, harmonic_number), 0)
    harmonic_rate = lax.broadcasted_iota(jnp.int32, (epoch_number, harmonic_number), 1)
    harmonic_offsets = (sample_moments * harmonic_rate % cycle_length).astype(jnp.float32) * (
        2.0 * math.pi / cycle_length
    )
    weight = (
        jnp.where((harmonic_rate == 0) | (harmonic_rate == harmonic_number - 1), 1.0, 2.0).astype(
            jnp.float32
        )
        / cycle_length
    )
    return jnp.concatenate(
        [weight * jnp.cos(harmonic_offsets), -weight * jnp.sin(harmonic_offsets)], axis=1
    )


def forward_table(epoch_number, harmonic_number):
    cycle_length = 2 * epoch_number
    harmonic_rate = lax.broadcasted_iota(jnp.int32, (harmonic_number, epoch_number), 0)
    sample_moments = lax.broadcasted_iota(jnp.int32, (harmonic_number, epoch_number), 1)
    harmonic_offsets = (sample_moments * harmonic_rate % cycle_length).astype(jnp.float32) * (
        2.0 * math.pi / cycle_length
    )
    return jnp.concatenate([jnp.cos(harmonic_offsets), -jnp.sin(harmonic_offsets)], axis=0)


def adjoint_product(columns, blocks):
    real_part = jnp.einsum("kjs,ksm->kjm", columns[0], blocks[0], precision=precise) + jnp.einsum(
        "kjs,ksm->kjm", columns[1], blocks[1], precision=precise
    )
    imag_part = jnp.einsum("kjs,ksm->kjm", columns[1], blocks[0], precision=precise) - jnp.einsum(
        "kjs,ksm->kjm", columns[0], blocks[1], precision=precise
    )
    return jnp.stack([real_part, imag_part])


def forward_product(spectrum, blocks):
    real_part = jnp.einsum("kjm,ksm->kjs", spectrum[0], blocks[0], precision=precise) - jnp.einsum(
        "kjm,ksm->kjs", spectrum[1], blocks[1], precision=precise
    )
    imag_part = jnp.einsum("kjm,ksm->kjs", spectrum[1], blocks[0], precision=precise) + jnp.einsum(
        "kjm,ksm->kjs", spectrum[0], blocks[1], precision=precise
    )
    return jnp.stack([real_part, imag_part])


def on_device(columns, freq_blocks, causal_cutoffs, band_index, band_rates):
    col_total = columns.shape[2]
    local_spectrum = adjoint_product(columns, freq_blocks)
    gathered = lax.all_to_all(local_spectrum, "freq", split_axis=2, concat_axis=1, tiled=True)
    freq_total = gathered.shape[1]
    horizon_span = freq_total - 1
    sampled_trace = jnp.dot(
        inverse_table(horizon_span, freq_total),
        gathered.reshape(2 * freq_total, MODE_SHARE_WIDTH * C_DEV),
        precision=precise,
        preferred_element_type=jnp.float32,
    )
    sampled_trace = sampled_trace.reshape(horizon_span, MODE_SHARE_WIDTH, C_DEV)
    device_ranges = lax.dynamic_slice_in_dim(
        causal_cutoffs, lax.axis_index("freq") * MODE_SHARE_WIDTH, MODE_SHARE_WIDTH
    )
    sample_moments = lax.broadcasted_iota(jnp.int32, (horizon_span, MODE_SHARE_WIDTH), 0)
    sampled_trace = jnp.where(
        (sample_moments < device_ranges[None, :])[:, :, None], sampled_trace, 0.0
    )
    flat = sampled_trace.reshape(horizon_span * MODE_SHARE_WIDTH, C_DEV)
    levels = lax.broadcasted_iota(jnp.int32, (BANDS, C_DEV), 0)
    cell_rates = jnp.sum(jnp.where(levels == band_index[None, :], band_rates[:, None], 0.0), axis=0)
    stacked = jnp.concatenate([flat, cell_rates[None, :]], axis=0)
    padded = extended(stacked, (("cell", 1),), SWEEPS)
    field = padded[:-1]
    margin_rates = padded[-1]
    for repeat in range(SWEEPS):
        inner_rates = margin_rates[1:-1]
        field = field[:, 1:-1] + inner_rates * (field[:, :-2] - 2.0 * field[:, 1:-1] + field[:, 2:])
        margin_rates = inner_rates
    flat = field
    spectrum = jnp.dot(
        forward_table(horizon_span, freq_total),
        flat.reshape(horizon_span, MODE_SHARE_WIDTH * C_DEV),
        precision=precise,
        preferred_element_type=jnp.float32,
    )
    spectrum = spectrum.reshape(2, freq_total, MODE_SHARE_WIDTH, C_DEV)
    returned = lax.all_to_all(spectrum, "freq", split_axis=1, concat_axis=2, tiled=True)
    partial_terms = forward_product(returned, freq_blocks)
    totals = lax.psum(partial_terms, "cell")
    share = col_total // lax.axis_size("cell")
    return lax.dynamic_slice_in_dim(totals, lax.axis_index("cell") * share, share, 2)


def solution(mesh):
    placed = (P(None, "freq", None, None), P(None, "freq", None, "cell"), P(), P("cell"), P())
    return jax.shard_map(
        on_device,
        mesh=mesh,
        in_specs=placed,
        out_specs=P(None, "freq", "cell", None),
        check_vma=False,
    )
```

profile of v0, /device:TPU:0, one launch (start us, length us, event | category | flops | bytes accessed | tf_op | source)
XLA Modules:
  0.0 98.5 jit_solution(15903029011630750266)
XLA Ops:
  6.5 2.4 %fusion.4 = f32[2,64,256]{2,1,0:T(8,128)S(1)} fusion(f32[2,2,600,256]{3,2,1,0:T(8,128)} %param.6, f32[2,2,64,600]{3,2,1,0:T(8,128)} %param.5), kind=kOutput, calls=%fused_computation.4 | convolution fusion | flops 235929600 | bytes 1687552 | tf_op jit(solution)/shard_map/kjs,ksm->kjm/dot_general | solution.py:59
  9.0 2.3 %fusion.6 = f32[2,64,256]{2,1,0:T(8,128)S(1)} fusion(f32[2,2,600,256]{3,2,1,0:T(8,128)} %param.6, f32[2,2,64,600]{3,2,1,0:T(8,128)} %param.5), kind=kOutput, calls=%fused_computation.6 | convolution fusion | flops 235929600 | bytes 1687552 | tf_op jit(solution)/shard_map/kjs,ksm->kjm/dot_general | solution.py:56
  11.4 0.9 fusion.37
  12.3 0.9 fusion.31
  13.2 0.9 copy.21
  14.1 7.3 %all-to-all-start = ((f32[2,2,64,256]{3,1,0,2:T(2,128)}), f32[2,2,64,256]{3,1,0,2:T(2,128)S(1)}, u32[]{:S(2)}, u32[]{:S(2)}) async-start(f32[2,2,64,256]{3,1,0,2:T(2,128)} %copy.21), calls=%async_computation | async-start | bytes 524288 | tf_op jit(solution)/shard_map/all_to_all | solution.py:78
  21.9 8.5 %all-to-all-done = f32[2,2,64,256]{3,1,0,2:T(2,128)S(1)} async-done(((f32[2,2,64,256]{3,1,0,2:T(2,128)}), f32[2,2,64,256]{3,1,0,2:T(2,128)S(1)}, u32[]{:S(2)}, u32[]{:S(2)}) %all-to-all-start) | async-done | bytes 262176 | tf_op jit(solution)/shard_map/all_to_all | solution.py:78
  30.4 0.3 convolution_select_fusion
  30.9 1.3 %collective-permute-start = (f32[121,4]{1,0:T(8,128)S(1)}, f32[121,4]{1,0:T(8,128)S(1)}, u32[]{:S(2)}, u32[]{:S(2)}) collective-permute-start(f32[121,4]{1,0:T(8,128)S(1)} %get-tuple-element.5), channel_id=1, source_target_pairs={{0,1},{1,2},{2,3},{4,5},{5,6},{6,7},{8,9},{9,10},{10,11},{12,13},{... | collective-permute-start | bytes 5816 | tf_op jit(solution)/shard_map/ppermute | solution.py:21
  32.2 1.3 %collective-permute-start.1 = (f32[121,4]{1,0:T(8,128)S(1)}, f32[121,4]{1,0:T(8,128)S(1)}, u32[]{:S(2)}, u32[]{:S(2)}) collective-permute-start(f32[121,4]{1,0:T(8,128)S(1)} %get-tuple-element.6), channel_id=1, source_target_pairs={{1,0},{2,1},{3,2},{5,4},{6,5},{7,6},{9,8},{10,9},{11,10},{13,12},{... | collective-permute-start | bytes 5816 | tf_op jit(solution)/shard_map/ppermute | solution.py:22
  33.5 3.5 %collective-permute-done.1 = f32[121,4]{1,0:T(8,128)S(1)} collective-permute-done((f32[121,4]{1,0:T(8,128)S(1)}, f32[121,4]{1,0:T(8,128)S(1)}, u32[]{:S(2)}, u32[]{:S(2)}) %collective-permute-start.1) | collective-permute-done | bytes 1968 | tf_op jit(solution)/shard_map/ppermute | solution.py:22
  37.3 0.2 fusion.63
  37.6 0.2 fusion.61
  37.8 0.2 fusion.59
  38.2 0.4 fusion.64
  38.6 0.2 copy.26
  38.8 11.7 %all_to_all.30 = f32[2,16,8,256]{3,2,0,1:T(8,128)S(1)} all-to-all(f32[2,16,8,256]{3,2,0,1:T(8,128)S(1)} %copy.26), channel_id=1, replica_groups=mesh['freq'=8,'cell'=4] {'freq'}, dimensions={1} | all-to-all | bytes 524288 | tf_op jit(solution)/shard_map/all_to_all | solution.py:114
  50.5 1.2 %fusion = f32[2,64,600]{2,1,0:T(8,128)S(1)} fusion(f32[2,2,600,256]{3,2,1,0:T(8,128)S(1)} %copy-done, f32[2,2,8,8,256]{4,3,2,1,0:T(8,128)S(1)} %bitcast.106), kind=kOutput, calls=%fused_computation | convolution fusion | flops 235929600 | bytes 1667072 | tf_op jit(solution)/shard_map/kjm,ksm->kjs/dot_general | solution.py:69
  51.7 1.2 %fusion.2 = f32[2,64,600]{2,1,0:T(8,128)S(1)} fusion(f32[2,2,600,256]{3,2,1,0:T(8,128)S(1)} %copy-done, f32[2,2,8,8,256]{4,3,2,1,0:T(8,128)S(1)} %bitcast.107), kind=kOutput, calls=%fused_computation.2 | convolution fusion | flops 235929600 | bytes 1667072 | tf_op jit(solution)/shard_map/kjm,ksm->kjs/dot_general | solution.py:66
  52.9 1.2 %fusion.22 = f32[1,2,64,600]{3,2,1,0:T(8,128)S(1)} fusion(f32[2,64,600]{2,1,0:T(8,128)S(1)} %fusion, f32[2,2,600,256]{3,2,1,0:T(8,128)S(1)} %copy-done, f32[2,2,8,8,256]{4,3,2,1,0:T(8,128)S(1)} %bitcast.108), kind=kOutput, calls=%fused_computation.18 | convolution fusion | flops 236006400 | bytes 1994752 | tf_op jit(solution)/shard_map/kjm,ksm->kjs/dot_general | solution.py:69
  54.2 1.2 %fusion.25 = f32[1,2,64,600]{3,2,1,0:T(8,128)S(1)} fusion(f32[2,64,600]{2,1,0:T(8,128)S(1)} %fusion.2, f32[2,2,600,256]{3,2,1,0:T(8,128)S(1)} %copy-done, f32[2,2,8,8,256]{4,3,2,1,0:T(8,128)S(1)} %bitcast.109), kind=kOutput, calls=%fused_computation.19 | convolution fusion | flops 236006400 | bytes 1994752 | tf_op jit(solution)/shard_map/kjm,ksm->kjs/dot_general | solution.py:66
  55.4 0.9 pad_maximum_fusion
  56.3 33.7 %all-reduce.2.cloned.1.call-done = f32[2,2,64,600]{3,2,1,0:T(8,128)} async-done(((f32[2,2,64,600]{3,2,1,0:T(8,128)}), f32[2,2,64,600]{3,2,1,0:T(8,128)}) %all-reduce.2.cloned.1.call-update) | async-done | bytes 614416 | tf_op jit(solution)/shard_map/psum | solution.py:116
  90.1 1.6 %constant_dynamic-slice_fusion = f32[2,2,16,600]{3,2,1,0:T(8,128)} fusion(f32[2,2,64,600]{3,2,1,0:T(8,128)} %all-reduce.2.cloned.1.call-done, s32[]{:T(128)S(6)} %select_n.44), kind=kLoop, calls=%fused_computation.104 | loop fusion | bytes 307204 | tf_op jit(solution)/shard_map/dynamic_slice | solution.py:118
  (34 shorter events, 1.3 us)
Async XLA Ops:
  6.5 4.8 %copy-start = (f32[2,2,600,256]{3,2,1,0:T(8,128)S(1)}, f32[2,2,600,256]{3,2,1,0:T(8,128)}, u32[]{:S(2)}) copy-start(f32[2,2,600,256]{3,2,1,0:T(8,128)} %param.6) | copy-start | bytes 7372804
  6.5 4.8 %copy-start.1 = (f32[2,2,64,600]{3,2,1,0:T(8,128)S(1)}, f32[2,2,64,600]{3,2,1,0:T(8,128)}, u32[]{:S(2)}) copy-start(f32[2,2,64,600]{3,2,1,0:T(8,128)} %param.5) | copy-start | bytes 1843204
  11.3 10.2 %copy-start.2 = (s32[256]{0:T(256)S(1)}, s32[256]{0:T(256)}, u32[]{:S(2)}) copy-start(s32[256]{0:T(256)} %param.8) | copy-start | bytes 3076
  11.3 10.2 %copy-start.3 = (f32[8]{0:T(128)S(1)}, f32[8]{0:T(128)}, u32[]{:S(2)}) copy-start(f32[8]{0:T(128)} %param.9) | copy-start | bytes 100
  11.3 10.3 %copy-start.4 = (s32[64]{0:T(128)S(1)}, s32[64]{0:T(128)}, u32[]{:S(2)}) copy-start(s32[64]{0:T(128)} %param.7) | copy-start | bytes 772
  14.1 16.2 %all-to-all-start = ((f32[2,2,64,256]{3,1,0,2:T(2,128)}), f32[2,2,64,256]{3,1,0,2:T(2,128)S(1)}, u32[]{:S(2)}, u32[]{:S(2)}) async-start(f32[2,2,64,256]{3,1,0,2:T(2,128)} %copy.21), calls=%async_computation | async-start | bytes 524288 | tf_op jit(solution)/shard_map/all_to_all | solution.py:78
  21.4 68.7 %all-reduce.2.cloned.1.call-start = ((), (), s32[]{:S(2)}) async-start(), calls=%async_computation.2 | async-start | bytes 1310720 | tf_op jit(solution)/shard_map/psum | solution.py:116
  30.9 2.6 %collective-permute-start = (f32[121,4]{1,0:T(8,128)S(1)}, f32[121,4]{1,0:T(8,128)S(1)}, u32[]{:S(2)}, u32[]{:S(2)}) collective-permute-start(f32[121,4]{1,0:T(8,128)S(1)} %get-tuple-element.5), channel_id=1, source_target_pairs={{0,1},{1,2},{2,3},{4,5},{5,6},{6,7},{8,9},{9,10},{10,11},{12,13},{... | collective-permute-start | bytes 5816 | tf_op jit(solution)/shard_map/ppermute | solution.py:21
  32.2 4.9 %collective-permute-start.1 = (f32[121,4]{1,0:T(8,128)S(1)}, f32[121,4]{1,0:T(8,128)S(1)}, u32[]{:S(2)}, u32[]{:S(2)}) collective-permute-start(f32[121,4]{1,0:T(8,128)S(1)} %get-tuple-element.6), channel_id=1, source_target_pairs={{1,0},{2,1},{3,2},{5,4},{6,5},{7,6},{9,8},{10,9},{11,10},{13,12},{... | collective-permute-start | bytes 5816 | tf_op jit(solution)/shard_map/ppermute | solution.py:22
Sparse Core Ops, SparseCore 0:
  56.5 33.5 all-reduce.1
where the time goes:
time: 98.8 us; the launch traced here: 98.5 us
  waiting for transfers between devices  45.8 us (46%)
  between operations  13.7 us (14%)
  matrix products  12.1 us (12%)
  blocking collectives  11.7 us (12%)
  starting transfers between devices  9.93 us (10%)
  local copies, waits for them, and re-layouts  2.98 us (3%)
  other arithmetic  2.33 us (2%)
    psum x1, waiting for transfers between devices, on_device(): totals = lax.psum(partial_terms, 'cell')  33.7 us
    all_to_all x1, blocking collectives, on_device(): lax.all_to_all(spectrum, 'freq', split_axis=1, concat_axis=2, tiled=True)  11.7 us
    all_to_all x1, waiting for transfers between devices, on_device(): lax.all_to_all(local_spectrum, 'freq', split_axis=2, concat_axis=1, tiled...  8.46 us
    all_to_all x1, starting transfers between devices, on_device(): lax.all_to_all(local_spectrum, 'freq', split_axis=2, concat_axis=1, tiled...  7.31 us
    ppermute x1, waiting for transfers between devices, extended(): after = lax.ppermute(leading, axis, down)  3.54 us
    dot_general x1, matrix products, adjoint_product(): jnp.einsum('kjs,ksm->kjm', columns[0], blocks[1], precision=precise)  2.44 us
    dot_general x1, matrix products, adjoint_product(): jnp.einsum('kjs,ksm->kjm', columns[1], blocks[1], precision=precise)  2.3 us
  transfers between devices with their start and end apart: 4, of which 3 were waited for; matrix products, arithmetic and copies ran while one was open for 0% of the time, Pallas kernels for 0%

commit v1 on v0

--- a/solution.py
+++ b/solution.py
@@ -113,7 +113,7 @@
     spectrum = spectrum.reshape(2, freq_total, MODE_SHARE_WIDTH, C_DEV)
     returned = lax.all_to_all(spectrum, "freq", split_axis=1, concat_axis=2, tiled=True)
     partial_terms = forward_product(returned, freq_blocks)
-    totals = lax.psum(partial_terms, "cell")
+    totals = lax.all_gather(partial_terms, "cell").sum(axis=0)
     share = col_total // lax.axis_size("cell")
     return lax.dynamic_slice_in_dim(totals, lax.axis_index("cell") * share, share, 2)
 

time: 98.8 us -> 91.4 us (0.925)
  waiting for transfers between devices: 45.8 us -> 37.3 us
  other arithmetic: 2.33 us -> 4.28 us
    psum x1 -> x0, waiting for transfers between devices: 33.7 us -> none  [on_device(): totals = lax.psum(partial_terms, 'cell')]
    all_gather x0 -> x1, waiting for transfers between devices: none -> 25.2 us  [on_device(): totals = lax.all_gather(partial_terms, 'cell').sum(axis=0)]
    reduce_sum x0 -> x1, other arithmetic: none -> 1.97 us  [on_device(): totals = lax.all_gather(partial_terms, 'cell').sum(axis=0)]
where the time goes in v1:
time: 91.4 us; the launch traced here: 91.1 us
  waiting for transfers between devices  37.3 us (41%)
  between operations  13.7 us (15%)
  matrix products  12.1 us (13%)
  blocking collectives  11.7 us (13%)
  starting transfers between devices  9.93 us (11%)
  other arithmetic  4.28 us (5%)
  local copies, waits for them, and re-layouts  2.07 us (2%)
    all_gather x1, waiting for transfers between devices, on_device(): totals = lax.all_gather(partial_terms, 'cell').sum(axis=0)  25.2 us
    all_to_all x1, blocking collectives, on_device(): lax.all_to_all(spectrum, 'freq', split_axis=1, concat_axis=2, tiled=True)  11.7 us
    all_to_all x1, waiting for transfers between devices, on_device(): lax.all_to_all(local_spectrum, 'freq', split_axis=2, concat_axis=1, tiled...  8.46 us
    all_to_all x1, starting transfers between devices, on_device(): lax.all_to_all(local_spectrum, 'freq', split_axis=2, concat_axis=1, tiled...  7.31 us
    ppermute x1, waiting for transfers between devices, extended(): after = lax.ppermute(leading, axis, down)  3.54 us
    dot_general x1, matrix products, adjoint_product(): jnp.einsum('kjs,ksm->kjm', columns[0], blocks[1], precision=precise)  2.44 us
    dot_general x1, matrix products, adjoint_product(): jnp.einsum('kjs,ksm->kjm', columns[1], blocks[1], precision=precise)  2.3 us
    reduce_sum x1, other arithmetic, on_device(): totals = lax.all_gather(partial_terms, 'cell').sum(axis=0)  1.97 us
  transfers between devices with their start and end apart: 4, of which 3 were waited for; matrix products, arithmetic and copies ran while one was open for 0% of the time, Pallas kernels for 0%

profile of v1, /device:TPU:0, one launch (start us, length us, event | category | flops | bytes accessed | tf_op | source)
XLA Modules:
  0.0 91.1 jit_solution(17092615549608225209)
XLA Ops:
  6.5 2.4 %fusion.4 = f32[2,64,256]{2,1,0:T(8,128)S(1)} fusion(f32[2,2,600,256]{3,2,1,0:T(8,128)} %param.6, f32[2,2,64,600]{3,2,1,0:T(8,128)} %param.5), kind=kOutput, calls=%fused_computation.4 | convolution fusion | flops 235929600 | bytes 1687552 | tf_op jit(solution)/shard_map/kjs,ksm->kjm/dot_general | solution.py:59
  9.0 2.3 %fusion.6 = f32[2,64,256]{2,1,0:T(8,128)S(1)} fusion(f32[2,2,600,256]{3,2,1,0:T(8,128)} %param.6, f32[2,2,64,600]{3,2,1,0:T(8,128)} %param.5), kind=kOutput, calls=%fused_computation.6 | convolution fusion | flops 235929600 | bytes 1687552 | tf_op jit(solution)/shard_map/kjs,ksm->kjm/dot_general | solution.py:56
  11.4 0.9 fusion.37
  12.3 0.9 fusion.31
  13.2 0.9 copy.21
  14.1 7.3 %all-to-all-start = ((f32[2,2,64,256]{3,1,0,2:T(2,128)}), f32[2,2,64,256]{3,1,0,2:T(2,128)S(1)}, u32[]{:S(2)}, u32[]{:S(2)}) async-start(f32[2,2,64,256]{3,1,0,2:T(2,128)} %copy.21), calls=%async_computation | async-start | bytes 524288 | tf_op jit(solution)/shard_map/all_to_all | solution.py:78
  21.9 8.5 %all-to-all-done = f32[2,2,64,256]{3,1,0,2:T(2,128)S(1)} async-done(((f32[2,2,64,256]{3,1,0,2:T(2,128)}), f32[2,2,64,256]{3,1,0,2:T(2,128)S(1)}, u32[]{:S(2)}, u32[]{:S(2)}) %all-to-all-start) | async-done | bytes 262176 | tf_op jit(solution)/shard_map/all_to_all | solution.py:78
  30.4 0.3 convolution_select_fusion
  30.9 1.3 %collective-permute-start = (f32[121,4]{1,0:T(8,128)S(1)}, f32[121,4]{1,0:T(8,128)S(1)}, u32[]{:S(2)}, u32[]{:S(2)}) collective-permute-start(f32[121,4]{1,0:T(8,128)S(1)} %get-tuple-element.5), channel_id=1, source_target_pairs={{0,1},{1,2},{2,3},{4,5},{5,6},{6,7},{8,9},{9,10},{10,11},{12,13},{... | collective-permute-start | bytes 5816 | tf_op jit(solution)/shard_map/ppermute | solution.py:21
  32.2 1.3 %collective-permute-start.1 = (f32[121,4]{1,0:T(8,128)S(1)}, f32[121,4]{1,0:T(8,128)S(1)}, u32[]{:S(2)}, u32[]{:S(2)}) collective-permute-start(f32[121,4]{1,0:T(8,128)S(1)} %get-tuple-element.6), channel_id=1, source_target_pairs={{1,0},{2,1},{3,2},{5,4},{6,5},{7,6},{9,8},{10,9},{11,10},{13,12},{... | collective-permute-start | bytes 5816 | tf_op jit(solution)/shard_map/ppermute | solution.py:22
  33.5 3.5 %collective-permute-done.1 = f32[121,4]{1,0:T(8,128)S(1)} collective-permute-done((f32[121,4]{1,0:T(8,128)S(1)}, f32[121,4]{1,0:T(8,128)S(1)}, u32[]{:S(2)}, u32[]{:S(2)}) %collective-permute-start.1) | collective-permute-done | bytes 1968 | tf_op jit(solution)/shard_map/ppermute | solution.py:22
  37.3 0.2 fusion.63
  37.6 0.2 fusion.61
  37.8 0.2 fusion.59
  38.2 0.4 fusion.64
  38.8 11.7 %all_to_all.30 = f32[2,16,8,256]{3,2,0,1:T(8,128)S(1)} all-to-all(f32[2,16,8,256]{3,2,0,1:T(8,128)S(1)} %copy.26), channel_id=1, replica_groups=mesh['freq'=8,'cell'=4] {'freq'}, dimensions={1} | all-to-all | bytes 524288 | tf_op jit(solution)/shard_map/all_to_all | solution.py:114
  50.5 1.2 %fusion = f32[2,64,600]{2,1,0:T(8,128)S(1)} fusion(f32[2,2,600,256]{3,2,1,0:T(8,128)S(1)} %copy-done, f32[2,2,8,8,256]{4,3,2,1,0:T(8,128)S(1)} %bitcast.108), kind=kOutput, calls=%fused_computation | convolution fusion | flops 235929600 | bytes 1667072 | tf_op jit(solution)/shard_map/kjm,ksm->kjs/dot_general | solution.py:69
  51.7 1.2 %fusion.2 = f32[2,64,600]{2,1,0:T(8,128)S(1)} fusion(f32[2,2,600,256]{3,2,1,0:T(8,128)S(1)} %copy-done, f32[2,2,8,8,256]{4,3,2,1,0:T(8,128)S(1)} %bitcast.109), kind=kOutput, calls=%fused_computation.2 | convolution fusion | flops 235929600 | bytes 1667072 | tf_op jit(solution)/shard_map/kjm,ksm->kjs/dot_general | solution.py:66
  52.9 1.2 %fusion.22 = f32[1,2,64,600]{3,2,1,0:T(8,128)S(1)} fusion(f32[2,64,600]{2,1,0:T(8,128)S(1)} %fusion, f32[2,2,600,256]{3,2,1,0:T(8,128)S(1)} %copy-done, f32[2,2,8,8,256]{4,3,2,1,0:T(8,128)S(1)} %bitcast.110), kind=kOutput, calls=%fused_computation.18 | convolution fusion | flops 236006400 | bytes 1994752 | tf_op jit(solution)/shard_map/kjm,ksm->kjs/dot_general | solution.py:69
  54.2 1.2 %fusion.25 = f32[1,2,64,600]{3,2,1,0:T(8,128)S(1)} fusion(f32[2,64,600]{2,1,0:T(8,128)S(1)} %fusion.2, f32[2,2,600,256]{3,2,1,0:T(8,128)S(1)} %copy-done, f32[2,2,8,8,256]{4,3,2,1,0:T(8,128)S(1)} %bitcast.111), kind=kOutput, calls=%fused_computation.19 | convolution fusion | flops 236006400 | bytes 1994752 | tf_op jit(solution)/shard_map/kjm,ksm->kjs/dot_general | solution.py:66
  55.4 0.9 pad_maximum_fusion
  56.3 25.2 %all-gather.3.cloned.1.call-done = f32[8,2,64,600]{3,2,1,0:T(8,128)} async-done(((f32[2,2,64,600]{3,2,1,0:T(8,128)}), f32[8,2,64,600]{3,2,1,0:T(8,128)}) %all-gather.3.cloned.1.call-update) | async-done | bytes 2457616 | tf_op jit(solution)/shard_map/all_gather | solution.py:116
  81.6 2.0 %reduce_sum.19 = f32[2,2,64,600]{3,2,1,0:T(8,128)S(1)} reduce(f32[4,2,2,64,600]{4,3,2,1,0:T(8,128)} %bitcast.107, f32[]{:T(128)} %constant.27.clone.1), dimensions={0}, to_apply=%region_1.2 | reduce | flops 460800 | bytes 3072004 | tf_op jit(solution)/shard_map/reduce_sum | solution.py:116
  83.5 0.7 constant_dynamic-slice_fusion
  (35 shorter events, 1.5 us)
Async XLA Ops:
  6.5 4.8 %copy-start = (f32[2,2,600,256]{3,2,1,0:T(8,128)S(1)}, f32[2,2,600,256]{3,2,1,0:T(8,128)}, u32[]{:S(2)}) copy-start(f32[2,2,600,256]{3,2,1,0:T(8,128)} %param.6) | copy-start | bytes 7372804
  6.5 4.8 %copy-start.1 = (f32[2,2,64,600]{3,2,1,0:T(8,128)S(1)}, f32[2,2,64,600]{3,2,1,0:T(8,128)}, u32[]{:S(2)}) copy-start(f32[2,2,64,600]{3,2,1,0:T(8,128)} %param.5) | copy-start | bytes 1843204
  11.3 10.2 %copy-start.2 = (s32[256]{0:T(256)S(1)}, s32[256]{0:T(256)}, u32[]{:S(2)}) copy-start(s32[256]{0:T(256)} %param.8) | copy-start | bytes 3076
  11.3 10.2 %copy-start.3 = (f32[8]{0:T(128)S(1)}, f32[8]{0:T(128)}, u32[]{:S(2)}) copy-start(f32[8]{0:T(128)} %param.9) | copy-start | bytes 100
  11.3 10.3 %copy-start.4 = (s32[64]{0:T(128)S(1)}, s32[64]{0:T(128)}, u32[]{:S(2)}) copy-start(s32[64]{0:T(128)} %param.7) | copy-start | bytes 772
  14.1 16.2 %all-to-all-start = ((f32[2,2,64,256]{3,1,0,2:T(2,128)}), f32[2,2,64,256]{3,1,0,2:T(2,128)S(1)}, u32[]{:S(2)}, u32[]{:S(2)}) async-start(f32[2,2,64,256]{3,1,0,2:T(2,128)} %copy.21), calls=%async_computation | async-start | bytes 524288 | tf_op jit(solution)/shard_map/all_to_all | solution.py:78
  21.4 60.2 %all-gather.3.cloned.1.call-start = ((), (), s32[]{:S(2)}) async-start(), calls=%async_computation.2 | async-start | bytes 3276800 | tf_op jit(solution)/shard_map/all_gather | solution.py:116
  30.9 2.6 %collective-permute-start = (f32[121,4]{1,0:T(8,128)S(1)}, f32[121,4]{1,0:T(8,128)S(1)}, u32[]{:S(2)}, u32[]{:S(2)}) collective-permute-start(f32[121,4]{1,0:T(8,128)S(1)} %get-tuple-element.5), channel_id=1, source_target_pairs={{0,1},{1,2},{2,3},{4,5},{5,6},{6,7},{8,9},{9,10},{10,11},{12,13},{... | collective-permute-start | bytes 5816 | tf_op jit(solution)/shard_map/ppermute | solution.py:21
  32.2 4.9 %collective-permute-start.1 = (f32[121,4]{1,0:T(8,128)S(1)}, f32[121,4]{1,0:T(8,128)S(1)}, u32[]{:S(2)}, u32[]{:S(2)}) collective-permute-start(f32[121,4]{1,0:T(8,128)S(1)} %get-tuple-element.6), channel_id=1, source_target_pairs={{1,0},{2,1},{3,2},{5,4},{6,5},{7,6},{9,8},{10,9},{11,10},{13,12},{... | collective-permute-start | bytes 5816 | tf_op jit(solution)/shard_map/ppermute | solution.py:22
Sparse Core Ops, SparseCore 0:
  56.4 25.0 all-gather.2
